TPU v7x, 32 devices: a whole 2x2x4 slice. The times are simulated.
32 devices in a mesh: tm: 16 (over z, y, core), series: 2 (over x).
Axes of the slice: x: 2, y: 2, z: 4, core: 2. Of those that a mesh axis runs over, the one named last changes fastest.
Arguments:
- history: bfloat16 [4, 4096, 1024], P('series', 'tm'), may hold values from -36 to 36
- lengths: int32 [4], P('series'), may hold values from 512 to 4096
- head_window: int32 [16], replicated, may hold values from 32 to 512, as said below
- input_proj: bfloat16 [1024, 3072], replicated
- output_proj: bfloat16 [1024, 1024], replicated, may hold values from -0.1875 to 0.1875
- mixer_down: bfloat16 [1024, 512], replicated, may hold values from -0.1875 to 0.1875
- mixer_up: bfloat16 [512, 1024], replicated, may hold values from -0.25 to 0.25
- series_mix: bfloat16 [4, 4], replicated, may hold values from -3 to 3
Outputs:
- layer_out: bfloat16 [4, 4096, 1024], P('series', 'tm')
Inputs may be any that keep to these rules, and one draw needn't show every extreme that they name: `head_window`: some head has exactly 512.
All inputs are finite; a program needn't handle non-finite values.
Results may differ from a plain program's by a relative error of at most 0.0065.
Values may be sent and summed in bfloat16 or wider, within the bound.
A program may use at most 128 MiB of HBM per device.

v0:
```python
import jax
import jax.numpy as jnp
from jax import lax
from jax.sharding import PartitionSpec as P

HEADS = 16
WINDOW = 512


def from_behind(block, axis, distance):
    devices = range(lax.axis_size(axis))
    route = [(i - distance, i) for i in devices if i - distance in devices]
    return lax.ppermute(block, axis, route)


def attend_series(queries, keys_values, length, head_window, query_first, key_first, patches):
    query_rows = queries.shape[0]
    model_width = queries.shape[1]
    key_rows = keys_values.shape[0]
    head_size = model_width // HEADS
    group_heads = min(4, HEADS)
    group_count = HEADS // group_heads
    group_width = group_heads * head_size
    query_pos = query_first + jnp.arange(query_rows, dtype=jnp.int32)
    key_pos = key_first + jnp.arange(key_rows, dtype=jnp.int32)
    key_valid = (key_pos >= patches - length) & (key_pos < patches)
    distance = jnp.abs(query_pos[:, None] - key_pos[None, :])

    def per_group(group_index):
        column = group_index * group_width
        group_queries = lax.dynamic_slice_in_dim(queries, column, group_width, 1).reshape(
            query_rows, group_heads, head_size
        )
        group_keys = lax.dynamic_slice_in_dim(keys_values, column, group_width, 1).reshape(
            key_rows, group_heads, head_size
        )
        group_values = lax.dynamic_slice_in_dim(
            keys_values, model_width + column, group_width, 1
        ).reshape(key_rows, group_heads, head_size)
        reaches = lax.dynamic_slice_in_dim(head_window, group_index * group_heads, group_heads, 0)
        scores = jnp.einsum(
            "qhd,khd->hqk", group_queries, group_keys, preferred_element_type=jnp.float32
        ) * head_size ** (-0.5)
        allowed = (distance[None, :, :] <= reaches[:, None, None]) & key_valid[None, None, :]
        scores = jnp.where(allowed, scores, -1e30)
        largest = jnp.max(scores, axis=-1, keepdims=True)
        weights = jnp.exp(scores - largest)
        totals = jnp.sum(weights, axis=-1)
        probabilities = weights.astype(jnp.bfloat16)
        combined = (
            jnp.einsum(
                "hqk,khd->qhd", probabilities, group_values, preferred_element_type=jnp.float32
            )
            / jnp.transpose(totals)[:, :, None]
        )
        return combined.reshape(query_rows, group_width)

    grouped = lax.map(per_group, jnp.arange(group_count, dtype=jnp.int32))
    combined = jnp.transpose(grouped, (1, 0, 2)).reshape(query_rows, model_width)
    query_valid = query_pos >= patches - length
    return jnp.where(query_valid[:, None], combined, 0.0).astype(jnp.bfloat16)


def on_device(
    history, lengths, head_window, input_proj, output_proj, mixer_down, mixer_up, series_mix
):
    local_series, local_patches, model_width = history.shape
    packed = jnp.einsum(
        "spd,de->spe", history, input_proj, preferred_element_type=jnp.float32
    ).astype(jnp.bfloat16)
    queries = packed[:, :, :model_width]
    keys_values = packed[:, :, model_width:]
    hops_count = -(-WINDOW // local_patches)
    earlier = []
    following = []
    kv_weight = input_proj[:, model_width:]
    for offset in range(1, hops_count + 1):
        before_rows = from_behind(history, "tm", offset)
        after_rows = from_behind(history, "tm", -offset)
        earlier.insert(
            0,
            jnp.einsum(
                "spd,de->spe", before_rows, kv_weight, preferred_element_type=jnp.float32
            ).astype(jnp.bfloat16),
        )
        following.append(
            jnp.einsum(
                "spd,de->spe", after_rows, kv_weight, preferred_element_type=jnp.float32
            ).astype(jnp.bfloat16)
        )
    context = jnp.concatenate(earlier + [keys_values] + following, axis=1)
    position = lax.axis_index("tm")
    patches = local_patches * lax.axis_size("tm")
    query_first = position * local_patches
    key_first = (position - hops_count) * local_patches

    def per_series(inputs):
        series_queries, series_context, length = inputs
        return attend_series(
            series_queries, series_context, length, head_window, query_first, key_first, patches
        )

    attended = lax.map(per_series, (queries, context, lengths))
    hidden = (
        history.astype(jnp.float32)
        + jnp.einsum("spd,de->spe", attended, output_proj, preferred_element_type=jnp.float32)
    ).astype(jnp.bfloat16)
    branch = jnp.einsum(
        "spd,dc->spc", hidden, mixer_down, preferred_element_type=jnp.float32
    ).astype(jnp.bfloat16)
    series_first = lax.axis_index("series") * local_series
    own_rows = lax.dynamic_slice_in_dim(series_mix, series_first, local_series, 0)
    combined = jnp.einsum(
        "ab,bpc->apc",
        own_rows,
        lax.all_gather(branch, "series", axis=0, tiled=True),
        preferred_element_type=jnp.float32,
    )
    combined = combined.astype(jnp.bfloat16)
    update = jnp.einsum("spc,cd->spd", combined, mixer_up, preferred_element_type=jnp.float32)
    return (hidden.astype(jnp.float32) + update).astype(jnp.bfloat16)


def solution(mesh):
    in_specs = (P("series", "tm", None), P("series"), P(), P(), P(), P(), P(), P())
    out_specs = P("series", "tm", None)
    return jax.shard_map(
        on_device, mesh=mesh, in_specs=in_specs, out_specs=out_specs, check_vma=False
    )
```

profile of v0, /device:TPU:4, one launch (start us, length us, event | category | flops | bytes accessed | tf_op | source)
XLA Modules:
  0.0 251.4 jit_solution(13896051567737535328)
XLA Ops:
  6.5 3.6 %collective-permute-start = (bf16[2,256,1024]{2,1,0:T(8,128)(2,1)}, bf16[2,256,1024]{2,1,0:T(8,128)(2,1)}, u32[]{:S(2)}, u32[]{:S(2)}) collective-permute-start(bf16[2,256,1024]{2,1,0:T(8,128)(2,1)} %param.12), channel_id=1, source_target_pairs={{0,4},{2,6},{4,8},{6,10},{8,12},{10,14},{12,16},{14,18},{16,20},{1... | collective-permute-start | bytes 3145736 | tf_op jit(solution)/shard_map/ppermute | solution.py:13
  10.1 1.9 collective-permute-start.1
  12.0 3.6 %collective-permute-start.2 = (bf16[2,256,1024]{2,1,0:T(8,128)(2,1)}, bf16[2,256,1024]{2,1,0:T(8,128)(2,1)}, u32[]{:S(2)}, u32[]{:S(2)}) collective-permute-start(bf16[2,256,1024]{2,1,0:T(8,128)(2,1)} %param.12), channel_id=1, source_target_pairs={{2,0},{4,2},{6,4},{8,6},{10,8},{12,10},{14,12},{16,14},{18,16},{20... | collective-permute-start | bytes 3145736 | tf_op jit(solution)/shard_map/ppermute | solution.py:13
  17.6 6.5 %fusion.22 = bf16[2,256,3072]{2,1,0:T(8,128)(2,1)S(1)} fusion(bf16[2,256,1024]{2,1,0:T(8,128)(2,1)} %param.12, bf16[1024,3072]{1,0:T(8,128)(2,1)} %param.15), kind=kOutput, calls=%fused_computation.29 | convolution fusion | flops 3222798336 | bytes 10485760 | tf_op jit(solution)/shard_map/spd,de->spe/dot_general | solution.py:68
  26.9 41.7 %collective-permute-done = bf16[2,256,1024]{2,1,0:T(8,128)(2,1)} collective-permute-done((bf16[2,256,1024]{2,1,0:T(8,128)(2,1)}, bf16[2,256,1024]{2,1,0:T(8,128)(2,1)}, u32[]{:S(2)}, u32[]{:S(2)}) %collective-permute-start) | collective-permute-done | bytes 1048608 | tf_op jit(solution)/shard_map/ppermute | solution.py:13
  68.6 5.0 %fusion.36 = bf16[2,1280,2048]{2,1,0:T(8,128)(2,1)S(1)} fusion(bf16[2,256,1024]{2,1,0:T(8,128)(2,1)} %collective-permute-done, bf16[1024,3072]{1,0:T(8,128)(2,1)} %param.15), kind=kOutput, calls=%fused_computation.39 | convolution fusion | flops 2148532224 | bytes 7340032 | tf_op jit(solution)/shard_map/spd,de->spe/dot_general | solution.py:82
  73.6 5.1 %collective-permute-done.1 = bf16[2,256,1024]{2,1,0:T(8,128)(2,1)} collective-permute-done((bf16[2,256,1024]{2,1,0:T(8,128)(2,1)}, bf16[2,256,1024]{2,1,0:T(8,128)(2,1)}, u32[]{:S(2)}, u32[]{:S(2)}) %collective-permute-start.1) | collective-permute-done | bytes 1048608 | tf_op jit(solution)/shard_map/ppermute | solution.py:13
  78.7 4.8 %fusion.42 = bf16[2,1280,2048]{2,1,0:T(8,128)(2,1)S(1)} fusion(bf16[2,1280,2048]{2,1,0:T(8,128)(2,1)S(1)} %fusion.36, bf16[2,256,1024]{2,1,0:T(8,128)(2,1)} %collective-permute-done.1, bf16[1024,3072]{1,0:T(8,128)(2,1)} %param.15), kind=kOutput, calls=%fused_computation.41 | convolution fusion | flops 2148532224 | bytes 7340032 | tf_op jit(solution)/shard_map/spd,de->spe/dot_general | solution.py:82
  83.8 3.6 %fusion.48 = bf16[2,1280,2048]{2,1,0:T(8,128)(2,1)S(1)} fusion(bf16[2,1280,2048]{2,1,0:T(8,128)(2,1)S(1)} %slice_dynamic-update-slice_fusion, bf16[2,256,1024]{2,1,0:T(8,128)(2,1)} %collective-permute-done.2, bf16[1024,3072]{1,0:T(8,128)(2,1)S(1)} %bitcast.116), kind=kOutput, calls=%fused_computation.43 | convolution fusion | flops 2148532224 | bytes 7340032 | tf_op jit(solution)/shard_map/spd,de->spe/dot_general | solution.py:87
  87.4 2.3 fusion.54
  89.7 4.0 %copy-done.1 = bf16[2,1280,2048]{2,1,0:T(8,128)(2,1)} copy-done((bf16[2,1280,2048]{2,1,0:T(8,128)(2,1)}, bf16[2,1280,2048]{2,1,0:T(8,128)(2,1)S(1)}, u32[]{:S(2)}) %copy-start.1) | copy-done | bytes 10485784
  93.7 118.7 %while.33 = (s32[]{:T(128)}, bf16[2,256,1024]{1,2,0:T(8,128)(2,1)}, s32[]{:T(128)}, s32[2]{0:T(128)S(1)}, bf16[2,256,1024]{2,1,0:T(8,128)(2,1)}, /*index=5*/bf16...) while((s32[]{:T(128)}, bf16[2,256,1024]{1,2,0:T(8,128)(2,1)}, ...), condition=%wide.region_5.6_spmd, body=%wide.region_0.5_spmd.sunk | while | flops 348394496 | bytes 47223572 | solution.py:103
  95.0 5.6 %constant_dynamic-slice_fusion.9 = bf16[1,1280,2048]{2,1,0:T(8,128)(2,1)} fusion(bf16[2,1280,2048]{2,1,0:T(8,128)(2,1)} %get-tuple-element.545, s32[]{:T(128)} %get-tuple-element.521), kind=kLoop, calls=%fused_computation.25.clone.1 | loop fusion | bytes 10485764 | tf_op jit(solution)/shard_map/while/body/jit(dynamic_index_in_dim)/dynamic_slice | solution.py:103
  100.6 7.9 %copy.26 = bf16[1,1280,2048]{1,2,0:T(8,128)(2,1)} copy(bf16[1,1280,2048]{2,1,0:T(8,128)(2,1)} %constant_dynamic-slice_fusion.9) | data formatting | bytes 10485760 | tf_op jit(solution)/shard_map/while/body/jit(dynamic_index_in_dim)/dynamic_slice | solution.py:103
  111.1 40.1 %while.34 = (s32[]{:T(128)}, bf16[4,256,256]{1,2,0:T(8,128)(2,1)}, s32[4]{0:T(128)}, bf16[1280,2048]{0,1:T(8,128)(2,1)}, s32[16]{0:T(128)}, /*index=5*/bf16[256,...) while((s32[]{:T(128)}, bf16[4,256,256]{1,2,0:T(8,128)(2,1)}, ...), condition=%wide.region_4.4_spmd.clone, body=%wide.region_1.3_spmd.clone.sunk | while | flops 348130304 | bytes 23098768 | solution.py:58
  151.1 1.9 fusion.92
  154.3 5.6 %constant_dynamic-slice_fusion.9 = bf16[1,1280,2048]{2,1,0:T(8,128)(2,1)} fusion(bf16[2,1280,2048]{2,1,0:T(8,128)(2,1)} %get-tuple-element.545, s32[]{:T(128)} %get-tuple-element.521), kind=kLoop, calls=%fused_computation.25.clone.1 | loop fusion | bytes 10485764 | tf_op jit(solution)/shard_map/while/body/jit(dynamic_index_in_dim)/dynamic_slice | solution.py:103
  159.9 7.9 %copy.26 = bf16[1,1280,2048]{1,2,0:T(8,128)(2,1)} copy(bf16[1,1280,2048]{2,1,0:T(8,128)(2,1)} %constant_dynamic-slice_fusion.9) | data formatting | bytes 10485760 | tf_op jit(solution)/shard_map/while/body/jit(dynamic_index_in_dim)/dynamic_slice | solution.py:103
  170.4 40.1 %while.34 = (s32[]{:T(128)}, bf16[4,256,256]{1,2,0:T(8,128)(2,1)}, s32[4]{0:T(128)}, bf16[1280,2048]{0,1:T(8,128)(2,1)}, s32[16]{0:T(128)}, /*index=5*/bf16[256,...) while((s32[]{:T(128)}, bf16[4,256,256]{1,2,0:T(8,128)(2,1)}, ...), condition=%wide.region_4.4_spmd.clone, body=%wide.region_1.3_spmd.clone.sunk | while | flops 348130304 | bytes 23098768 | solution.py:58
  210.5 1.9 fusion.92
  212.4 3.0 %add_convert_fusion.1 = bf16[2,256,1024]{2,1,0:T(8,128)(2,1)S(1)} fusion(bf16[2,256,1024]{2,1,0:T(8,128)(2,1)} %param.12, bf16[2,256,1024]{1,2,0:T(8,128)(2,1)} %get-tuple-element.223, bf16[1024,1024]{1,0:T(8,128)(2,1)S(1)} %copy-done), kind=kOutput, calls=%fused_computation.54 | convolution fusion | flops 1075314688 | bytes 5242880 | tf_op jit(solution)/shard_map/spd,de->spe/dot_general | solution.py:106
  217.9 21.6 %all-gather.2.cloned.1.call-done = bf16[4,256,512]{2,1,0:T(8,128)(2,1)} async-done(((bf16[2,256,512]{2,1,0:T(8,128)(2,1)}), bf16[4,256,512]{2,1,0:T(8,128)(2,1)}) %all-gather.2.cloned.1.call-update) | async-done | bytes 1048592 | tf_op jit(solution)/shard_map/all_gather | solution.py:116
  239.5 2.1 fusion.67
  241.7 2.9 %add_convert_fusion = bf16[2,256,1024]{2,1,0:T(8,128)(2,1)} fusion(bf16[2,256,1024]{2,1,0:T(8,128)(2,1)} %copy-done.8, bf16[512,1024]{1,0:T(8,128)(2,1)S(1)} %copy-done.5, bf16[2,256,512]{2,0,1:T(2,128)(2,1)S(1)} %fusion.67), kind=kOutput, calls=%fused_computation.53 | convolution fusion | flops 538443776 | bytes 3670016 | tf_op jit(solution)/shard_map/spc,cd->spd/dot_general | solution.py:120
  (127 shorter events, 84.4 us)
Async XLA Ops:
  6.5 205.9 %copy-start = (bf16[1024,1024]{1,0:T(8,128)(2,1)S(1)}, bf16[1024,1024]{1,0:T(8,128)(2,1)}, u32[]{:S(2)}) copy-start(bf16[1024,1024]{1,0:T(8,128)(2,1)} %param.16) | copy-start | bytes 6291460
  6.5 233.0 %all-gather.2.cloned.1.call-start = ((), (), s32[]{:S(2)}) async-start(), calls=%async_computation | async-start | bytes 1572864 | tf_op jit(solution)/shard_map/all_gather | solution.py:116
  6.5 62.1 %collective-permute-start = (bf16[2,256,1024]{2,1,0:T(8,128)(2,1)}, bf16[2,256,1024]{2,1,0:T(8,128)(2,1)}, u32[]{:S(2)}, u32[]{:S(2)}) collective-permute-start(bf16[2,256,1024]{2,1,0:T(8,128)(2,1)} %param.12), channel_id=1, source_target_pairs={{0,4},{2,6},{4,8},{6,10},{8,12},{10,14},{12,16},{14,18},{16,20},{1... | collective-permute-start | bytes 3145736 | tf_op jit(solution)/shard_map/ppermute | solution.py:13
  10.1 68.6 %collective-permute-start.1 = (bf16[2,256,1024]{2,1,0:T(8,128)(2,1)}, bf16[2,256,1024]{2,1,0:T(8,128)(2,1)}, u32[]{:S(2)}, u32[]{:S(2)}) collective-permute-start(bf16[2,256,1024]{2,1,0:T(8,128)(2,1)} %param.12), channel_id=1, source_target_pairs={{0,2},{2,4},{4,6},{6,8},{8,10},{10,12},{12,14},{14,16},{16,18},{18... | collective-permute-start | bytes 3145736 | tf_op jit(solution)/shard_map/ppermute | solution.py:13
  12.0 71.7 %collective-permute-start.2 = (bf16[2,256,1024]{2,1,0:T(8,128)(2,1)}, bf16[2,256,1024]{2,1,0:T(8,128)(2,1)}, u32[]{:S(2)}, u32[]{:S(2)}) collective-permute-start(bf16[2,256,1024]{2,1,0:T(8,128)(2,1)} %param.12), channel_id=1, source_target_pairs={{2,0},{4,2},{6,4},{8,6},{10,8},{12,10},{14,12},{16,14},{18,16},{20... | collective-permute-start | bytes 3145736 | tf_op jit(solution)/shard_map/ppermute | solution.py:13
  15.7 71.7 %collective-permute-start.3 = (bf16[2,256,1024]{2,1,0:T(8,128)(2,1)}, bf16[2,256,1024]{2,1,0:T(8,128)(2,1)S(1)}, u32[]{:S(2)}, u32[]{:S(2)}) collective-permute-start(bf16[2,256,1024]{2,1,0:T(8,128)(2,1)} %param.12), channel_id=1, source_target_pairs={{4,0},{6,2},{8,4},{10,6},{12,8},{14,10},{16,12},{18,14},{20,16},{2... | collective-permute-start | bytes 3145736 | tf_op jit(solution)/shard_map/ppermute | solution.py:13
  24.2 1.6 copy-start.2
  68.6 15.2 %slice-start = ((s8[6291456]{0:T(1024)(128)(4,1)}), s8[4194304]{0:T(1024)(128)(4,1)S(1)}, s32[]{:S(2)}) async-start(s8[6291456]{0:T(1024)(128)(4,1)} %bitcast.115), calls=%async_computation.1 | async-start | bytes 8388608
  73.6 10.0 %copy-start.3 = (bf16[2,256,3072]{2,1,0:T(8,128)(2,1)S(1)}, bf16[2,256,3072]{2,1,0:T(8,128)(2,1)}, u32[]{:S(2)}) copy-start(bf16[2,256,3072]{2,1,0:T(8,128)(2,1)} %copy-done.2) | copy-start | bytes 9437188
  73.6 10.2 %slice-start.1 = ((s8[6291456]{0:T(1024)(128)(4,1)}), s8[2097152]{0:T(1024)(128)(4,1)S(1)}, s32[]{:S(2)}) async-start(s8[6291456]{0:T(1024)(128)(4,1)} %bitcast.115), calls=%async_computation.2 | async-start | bytes 4194304
  87.4 6.4 %copy-start.7 = (s32[2]{0:T(128)S(1)}, s32[2]{0:T(128)}, u32[]{:S(2)}) copy-start(s32[2]{0:T(128)} %param.13) | copy-start | bytes 28
  89.7 4.0 %copy-start.1 = (bf16[2,1280,2048]{2,1,0:T(8,128)(2,1)}, bf16[2,1280,2048]{2,1,0:T(8,128)(2,1)S(1)}, u32[]{:S(2)}) copy-start(bf16[2,1280,2048]{2,1,0:T(8,128)(2,1)S(1)} %fusion.54) | copy-start | bytes 31457284
  212.4 4.0 %copy-start.4 = (bf16[1024,512]{1,0:T(8,128)(2,1)S(1)}, bf16[1024,512]{1,0:T(8,128)(2,1)}, u32[]{:S(2)}) copy-start(bf16[1024,512]{1,0:T(8,128)(2,1)} %param.17) | copy-start | bytes 3145732
  212.4 27.1 %copy-start.6 = (bf16[4,4]{1,0:T(4,128)(2,1)S(1)}, bf16[4,4]{1,0:T(4,128)(2,1)}, u32[]{:S(2)}) copy-start(bf16[4,4]{1,0:T(4,128)(2,1)} %param.19) | copy-start | bytes 100
  212.4 29.2 %copy-start.5 = (bf16[512,1024]{1,0:T(8,128)(2,1)S(1)}, bf16[512,1024]{1,0:T(8,128)(2,1)}, u32[]{:S(2)}) copy-start(bf16[512,1024]{1,0:T(8,128)(2,1)} %param.18) | copy-start | bytes 3145732
  215.4 1.0 copy-start.8
Sparse Core Ops, SparseCore 0:
  218.0 21.4 all-gather.1
where the time goes:
time: 255 us; the launch traced here: 251 us
  local copies, waits for them, and re-layouts  80 us (31%)
  waiting for transfers between devices  68.5 us (27%)
  matrix products  53.9 us (21%)
  other arithmetic  13.6 us (5%)
  between operations  13.6 us (5%)
  starting transfers between devices  11 us (4%)
  loops' own time  10.8 us (4%)
    ppermute x4, waiting for transfers between devices, from_behind(): return lax.ppermute(block, axis, route)  46.8 us
    dynamic_slice x10, local copies, waits for them, and re-layouts, on_device(): attended = lax.map(per_series, (queries, context, lengths))  32.4 us
    all_gather x1, waiting for transfers between devices, on_device(): lax.all_gather(branch, 'series', axis=0, tiled=True)  21.6 us
    dot_general x8, matrix products, per_group(): jnp.einsum('qhd,khd->hqk', group_queries, group_keys, preferred_element_t...  14.1 us
    ppermute x4, starting transfers between devices, from_behind(): return lax.ppermute(block, axis, route)  11 us
    dynamic_slice x8, local copies, waits for them, and re-layouts, per_group(): lax.dynamic_slice_in_dim(keys_values, column, group_width, 1)  11 us
    dot_general x2, matrix products, on_device(): jnp.einsum('spd,de->spe', before_rows, kv_weight, preferred_element_type=...  9.83 us
    another operation x2, loops' own time, attend_series(): grouped = lax.map(per_group, jnp.arange(group_count, dtype=jnp.int32))  9.47 us
  transfers between devices with their start and end apart: 5, of which 3 were waited for; matrix products, arithmetic and copies ran while one was open for 8% of the time, Pallas kernels for 0%

commit v1 on v0

v1 whole, which is shorter than its diff:
```python
import functools

import jax
import jax.numpy as jnp
from jax import lax
from jax.experimental import pallas as pl
from jax.experimental.pallas import tpu as pltpu
from jax.sharding import PartitionSpec as P

HEADS = 16
WINDOW = 512
BLOCK = 128
MASKED = -1e30
PIECES = 4
MESH = pl.DeviceIdType.MESH


def exchange_kernel(
    history_ref, weight_hbm, queries_ref, context_ref,
    halo, weight, weight_sem, partner_send, partner_recv, y_send, y_recv,
    z_send, z_recv, x_send, x_recv, *, scale,
):
    series, rows, width = history_ref.shape
    tiles = 6
    tile = weight.shape[1] // tiles
    piece = rows // PIECES
    me = lax.axis_index("tm")
    count = lax.axis_size("tm")
    core = me % 2
    side = (me // 2) % 2
    partner = me + 1 - 2 * core
    across = me + 2 - 4 * side
    onward = me + 4 - 8 * side
    origin = me - 4 + 8 * side
    has_onward = (onward >= 0) & (onward < count)
    has_origin = (origin >= 0) & (origin < count)

    loads = [
        pltpu.make_async_copy(
            weight_hbm.at[:, pl.ds(t * tile, tile)],
            weight.at[:, pl.ds(t * tile, tile)],
            weight_sem.at[t],
        )
        for t in range(tiles)
    ]
    for load in loads[2:] + loads[:2]:
        load.start()

    barrier = pltpu.get_barrier_semaphore()
    for other in (partner, across):
        pl.semaphore_signal(barrier, inc=1, device_id={"tm": other}, device_id_type=MESH)
    for other, exists in ((onward, has_onward), (origin, has_origin)):
        @pl.when(exists)
        def _():
            pl.semaphore_signal(barrier, inc=1, device_id={"tm": other}, device_id_type=MESH)
    peers = 2 + jnp.where(has_onward, 1, 0) + jnp.where(has_origin, 1, 0)
    pl.semaphore_wait(barrier, peers)

    def remote(source, target, send, recv, device):
        return pltpu.make_async_remote_copy(
            src_ref=source, dst_ref=target, send_sem=send, recv_sem=recv,
            device_id={"tm": device}, device_id_type=MESH,
        )

    def y_copy(s, r):
        part = pl.ds(r * piece, piece)
        return remote(
            history_ref.at[s, part, :], halo.at[1, s, part, :],
            y_send.at[s, r], y_recv.at[s, r], across,
        )

    def z_copy(s, r):
        part = pl.ds(r * piece, piece)
        return remote(
            halo.at[1, s, part, :], halo.at[2, s, part, :],
            z_send.at[s, r], z_recv.at[s, r], onward,
        )

    def partner_copy(s):
        return remote(
            history_ref.at[s], halo.at[0, s], partner_send.at[s], partner_recv.at[s], partner
        )

    def x_copy(s, role):
        return remote(halo.at[role, s], halo.at[3, s], x_send.at[s], x_recv.at[s], partner)

    for s in range(series):
        for r in range(PIECES):
            y_copy(s, r).start()
        partner_copy(s).start()

    @pl.when(jnp.logical_not(has_origin))
    def _():
        halo[2] = jnp.zeros(halo.shape[1:], halo.dtype)

    def project(source, s, slot):
        first = pl.multiple_of(slot * rows, rows)

        def body(t, _):
            column = pl.multiple_of(t * tile, tile)
            out = jnp.dot(
                source[...], weight[:, pl.ds(width + column, tile)],
                preferred_element_type=jnp.float32,
            )
            context_ref[s, pl.ds(first, rows), pl.ds(column, tile)] = out.astype(jnp.bfloat16)
            return 0

        lax.fori_loop(0, 2 * width // tile, body, 0)

    def project_queries(s):
        def body(t, _):
            column = pl.multiple_of(t * tile, tile)
            out = jnp.dot(
                history_ref[s], weight[:, pl.ds(column, tile)],
                preferred_element_type=jnp.float32,
            )
            queries_ref[s, :, pl.ds(column, tile)] = out.astype(jnp.bfloat16) * scale
            return 0

        lax.fori_loop(0, width // tile, body, 0)

    def relay(s, r):
        y_copy(s, r).wait_recv()

        @pl.when(has_onward)
        def _():
            z_copy(s, r).start()

    near = core == side
    slot_partner = 3 - 2 * core
    slot_a = 4 - 4 * side
    slot_b = 4 * side
    slot_x = 1 + 2 * core

    def finish_a(s):
        @pl.when(near)
        def _():
            x_copy(s, 1).start()
        project(halo.at[1, s], s, slot_a)

    def finish_b(s):
        @pl.when(has_origin)
        def _():
            for r in range(PIECES):
                z_copy(s, r).wait_recv()

        @pl.when(jnp.logical_not(near))
        def _():
            x_copy(s, 2).start()
        project(halo.at[2, s], s, slot_b)

    def finish_x(s):
        x_copy(s, 1).wait_recv()
        project(halo.at[3, s], s, slot_x)

    for load in loads[2:]:
        load.wait()
    project(history_ref.at[0], 0, 2)
    for load in loads[:2]:
        load.wait()
    project_queries(0)
    relay(0, 0)
    project(history_ref.at[1], 1, 2)
    project_queries(1)
    relay(0, 1)
    for s in range(series):
        partner_copy(s).wait_recv()
        project(halo.at[0, s], s, slot_partner)
    relay(0, 2)
    relay(0, 3)
    finish_a(0)
    relay(1, 0)
    finish_b(0)
    relay(1, 1)
    finish_x(0)
    relay(1, 2)
    relay(1, 3)
    finish_a(1)
    finish_b(1)
    finish_x(1)

    for s in range(series):
        partner_copy(s).wait_send()
        x_copy(s, 1).wait_send()
        for r in range(PIECES):
            y_copy(s, r).wait_send()

    @pl.when(has_onward)
    def _():
        for s in range(series):
            for r in range(PIECES):
                z_copy(s, r).wait_send()


def attention_kernel(lengths_ref, window_ref, queries_ref, context_ref, out_ref, bias_ref, *, hops):
    series, rows, width = queries_ref.shape
    keys = context_ref.shape[1]
    head_size = width // HEADS
    pairs = width // BLOCK
    reach = WINDOW // BLOCK
    me = lax.axis_index("tm")
    patches = rows * lax.axis_size("tm")
    first = me * rows - hops * rows
    center = hops * rows // BLOCK
    key_pos = first + lax.broadcasted_iota(jnp.int32, (1, keys), 1)
    query_pos = me * rows + lax.broadcasted_iota(jnp.int32, (rows, BLOCK), 0)

    for s in range(series):
        start = patches - lengths_ref[s]
        bias_ref[s] = jnp.where((key_pos >= start) & (key_pos < patches), 0.0, MASKED)

    def one_head(s, pair, half, steps, window):
        column = pl.multiple_of(pair * BLOCK, BLOCK)
        lane = lax.broadcasted_iota(jnp.int32, (BLOCK, BLOCK), 1)
        tilt = lane - lax.broadcasted_iota(jnp.int32, (BLOCK, BLOCK), 0)
        mine = (lane // head_size) == half
        span = (2 * steps + 1) * BLOCK
        for part in range(rows // BLOCK):
            low = (center + part - steps) * BLOCK
            q = queries_ref[s, part * BLOCK : (part + 1) * BLOCK, pl.ds(column, BLOCK)]
            q = jnp.where(mine, q, jnp.zeros_like(q))
            k = context_ref[s, low : low + span, pl.ds(column, BLOCK)]
            scores = lax.dot_general(
                q, k, (((1,), (1,)), ((), ())), preferred_element_type=jnp.float32
            )
            chunks = []
            for o in range(-steps, steps + 1):
                at = (o + steps) * BLOCK
                chunk = scores[:, at : at + BLOCK] + bias_ref[s, :, low + at : low + at + BLOCK]
                if abs(o) >= steps - 1:
                    if o <= 0:
                        chunk = jnp.where(tilt >= -(window + o * BLOCK), chunk, MASKED)
                    if o >= 0:
                        chunk = jnp.where(tilt <= window - o * BLOCK, chunk, MASKED)
                chunks.append(chunk)
            top = chunks[0]
            for chunk in chunks[1:]:
                top = jnp.maximum(top, chunk)
            top = jnp.max(top, axis=1, keepdims=True)
            weights = jnp.concatenate(
                [jnp.exp(chunk - top).astype(jnp.bfloat16) for chunk in chunks], axis=1
            )
            v = context_ref[s, low : low + span, pl.ds(width + column, BLOCK)]
            v = jnp.concatenate([v, jnp.ones((span, BLOCK), jnp.bfloat16)], axis=1)
            both = jnp.dot(weights, v, preferred_element_type=jnp.float32)
            result = both[:, :BLOCK] / both[:, BLOCK:]
            here = query_pos[part * BLOCK : (part + 1) * BLOCK]
            result = jnp.where(here >= patches - lengths_ref[s], result, 0.0).astype(jnp.bfloat16)
            place = (s, slice(part * BLOCK, (part + 1) * BLOCK), pl.ds(column, BLOCK))
            if half:
                result = jnp.where(mine, result, out_ref[place])
            out_ref[place] = result

    def body(index, _):
        s = index // pairs
        pair = index % pairs
        for half in range(BLOCK // head_size):
            window = window_ref[pair * (BLOCK // head_size) + half]
            needed = (window + BLOCK - 1) // BLOCK
            for steps in range(1, reach + 1):
                @pl.when(needed == steps)
                def _():
                    one_head(s, pair, half, steps, window)
        return 0

    lax.fori_loop(0, series * pairs, body, 0)


def on_device(
    history, lengths, head_window, input_proj, output_proj, mixer_down, mixer_up, series_mix
):
    series, rows, width = history.shape
    hops = -(-WINDOW // rows)
    keys = (2 * hops + 1) * rows
    head_size = width // HEADS
    vmem = pl.BlockSpec(memory_space=pltpu.VMEM)
    smem = pl.BlockSpec(memory_space=pltpu.SMEM)
    dma = pltpu.SemaphoreType.DMA
    queries, context = pl.pallas_call(
        functools.partial(exchange_kernel, scale=head_size ** (-0.5)),
        out_shape=(
            jax.ShapeDtypeStruct((series, rows, width), jnp.bfloat16),
            jax.ShapeDtypeStruct((series, keys, 2 * width), jnp.bfloat16),
        ),
        in_specs=[vmem, pl.BlockSpec(memory_space=pltpu.HBM)],
        out_specs=(vmem, vmem),
        scratch_shapes=[
            pltpu.VMEM((4, series, rows, width), jnp.bfloat16),
            pltpu.VMEM(input_proj.shape, jnp.bfloat16),
            dma((6,)),
            dma((series,)),
            dma((series,)),
            dma((series, PIECES)),
            dma((series, PIECES)),
            dma((series, PIECES)),
            dma((series, PIECES)),
            dma((series,)),
            dma((series,)),
        ],
        compiler_params=pltpu.CompilerParams(
            collective_id=0, has_side_effects=True, vmem_limit_bytes=32 * 1024 * 1024
        ),
    )(history, input_proj)
    attended = pl.pallas_call(
        functools.partial(attention_kernel, hops=hops),
        out_shape=jax.ShapeDtypeStruct((series, rows, width), jnp.bfloat16),
        in_specs=[smem, smem, vmem, vmem],
        out_specs=vmem,
        scratch_shapes=[pltpu.VMEM((series, 1, keys), jnp.float32)],
        compiler_params=pltpu.CompilerParams(vmem_limit_bytes=32 * 1024 * 1024),
    )(lengths, head_window, queries, context)
    hidden = (
        history.astype(jnp.float32)
        + jnp.einsum("spd,de->spe", attended, output_proj, preferred_element_type=jnp.float32)
    ).astype(jnp.bfloat16)
    branch = jnp.einsum(
        "spd,dc->spc", hidden, mixer_down, preferred_element_type=jnp.float32
    ).astype(jnp.bfloat16)
    groups = lax.axis_size("series")
    group = lax.axis_index("series")
    own_rows = lax.dynamic_slice_in_dim(series_mix, group * series, series, 0)

    def mixed(part, source):
        share = lax.dynamic_slice_in_dim(own_rows, source * series, series, 1)
        return jnp.einsum("ab,bpc->apc", share, part, preferred_element_type=jnp.float32)

    combined = mixed(branch, group)
    for offset in range(1, groups):
        route = [(i, (i + offset) % groups) for i in range(groups)]
        part = lax.ppermute(branch, "series", route)
        combined = combined + mixed(part, (group - offset) % groups)
    combined = combined.astype(jnp.bfloat16)
    update = jnp.einsum("spc,cd->spd", combined, mixer_up, preferred_element_type=jnp.float32)
    return (hidden.astype(jnp.float32) + update).astype(jnp.bfloat16)


def solution(mesh):
    in_specs = (P("series", "tm", None), P("series"), P(), P(), P(), P(), P(), P())
    out_specs = P("series", "tm", None)
    return jax.shard_map(
        on_device, mesh=mesh, in_specs=in_specs, out_specs=out_specs, check_vma=False
    )
```

time: 255 us -> 89.5 us (0.35); the launches traced: 251 us -> 90.2 us
  local copies, waits for them, and re-layouts: 80 us -> 5.16 us
  Pallas kernels: 0 us -> 64.3 us
  waiting for transfers between devices: 68.5 us -> 10.9 us
  matrix products: 53.9 us -> 8.27 us
  other arithmetic: 13.6 us -> 0 us
  between operations: 13.6 us -> 0.11 us
  loops' own time: 10.8 us -> 0 us
  starting transfers between devices: 11 us -> 1.49 us
    dynamic_slice x42 -> x0, local copies, waits for them, and re-layouts: 65.9 us -> none  [the longest x10 32.4 us: on_device(): attended = lax.map(per_series, (queries, context, lengths))]
    pallas_call x0 -> x2, Pallas kernels: none -> 64.3 us  [the longest x1 37.5 us: on_device(): pl.pallas_call(functools.partial(exchange_kernel, scale=head_size ** (-0....]
    dot_general x22 -> x2, matrix products: 46.5 us -> 3.68 us  [mixed(): jnp.einsum('ab,bpc->apc', share, part, preferred_element_type=jnp.float32)]
    ppermute x4 -> x1, waiting for transfers between devices: 46.8 us -> 10.9 us  [on_device(): part = lax.ppermute(branch, 'series', route)]
    all_gather x1 -> x0, waiting for transfers between devices: 21.6 us -> none  [on_device(): lax.all_gather(branch, 'series', axis=0, tiled=True)]
    another operation x3 -> x0, loops' own time: 10.8 us -> none  [the longest x2 9.47 us: attend_series(): grouped = lax.map(per_group, jnp.arange(group_count, dtype=jnp.int32))]
    ppermute x4 -> x1, starting transfers between devices: 11 us -> 1.49 us  [on_device(): part = lax.ppermute(branch, 'series', route)]
    reduce_sum x8 -> x0, other arithmetic: 7.71 us -> none  [per_group(): totals = jnp.sum(weights, axis=-1)]
  transfers between devices with their start and end apart: 5 -> 1, of which waited for: 3 -> 1; matrix products, arithmetic and copies ran while one was open for 8% -> 2% of each run, Pallas kernels for 0% -> 0%
where the time goes in v1:
time: 89.5 us; the launch traced here: 90.2 us
  Pallas kernels  64.3 us (72%)
  waiting for transfers between devices  10.9 us (12%)
  matrix products  8.27 us (9%)
  local copies, waits for them, and re-layouts  5.16 us (6%)
  starting transfers between devices  1.49 us (2%)
    pallas_call x1, Pallas kernels, on_device(): pl.pallas_call(functools.partial(exchange_kernel, scale=head_size ** (-0....  37.5 us
    pallas_call x1, Pallas kernels, on_device(): pl.pallas_call(functools.partial(attention_kernel, hops=hops), out_shape=...  26.8 us
    ppermute x1, waiting for transfers between devices, on_device(): part = lax.ppermute(branch, 'series', route)  10.9 us
    unnamed x22, local copies, waits for them, and re-layouts  5.16 us
    dot_general x2, matrix products, mixed(): jnp.einsum('ab,bpc->apc', share, part, preferred_element_type=jnp.float32)  3.68 us
    dot_general x1, matrix products, on_device(): jnp.einsum('spc,cd->spd', combined, mixer_up, preferred_element_type=jnp....  1.81 us
  transfers between devices with their start and end apart: 1, of which 1 were waited for; matrix products, arithmetic and copies ran while one was open for 2% of the time, Pallas kernels for 0%

profile of v1, /device:TPU:4, one launch (start us, length us, event | category | flops | bytes accessed | tf_op | source)
XLA Modules:
  0.0 90.2 jit_solution(14096910052089066962)
XLA Ops:
  0.0 0.0 copy-start
  0.0 2.9 %copy-done.1 = bf16[1024,3072]{1,0:T(8,128)(2,1)S(1)} copy-done((bf16[1024,3072]{1,0:T(8,128)(2,1)S(1)}, bf16[1024,3072]{1,0:T(8,128)(2,1)}, u32[]{:S(2)}) %copy-start.1) | copy-done | bytes 6291480
  2.9 1.2 %copy-done.2 = bf16[2,256,1024]{2,1,0:T(8,128)(2,1)S(1)} copy-done((bf16[2,256,1024]{2,1,0:T(8,128)(2,1)S(1)}, bf16[2,256,1024]{2,1,0:T(8,128)(2,1)}, u32[]{:S(2)}) %copy-start.2) | copy-done | bytes 1048600
  4.2 37.5 %shard_map.82 = (bf16[2,256,1024]{2,1,0:T(8,128)(2,1)S(1)}, bf16[2,1280,2048]{2,1,0:T(8,128)(2,1)S(1)}) custom-call(bf16[2,256,1024]{2,1,0:T(8,128)(2,1)S(1)} %copy-done.2, bf16[1024,3072]{1,0:T(8,128)(2,1)S(1)} %copy-done.1), custom_call_target="tpu_custom_call" | custom-call | tf_op jit(solution)/shard_map/pallas_call | solution.py:279
  41.7 0.0 copy-done.4
  41.7 0.0 copy-done.5
  41.7 0.0 copy-start.3
  41.7 26.8 %shard_map.83 = bf16[2,256,1024]{2,1,0:T(8,128)(2,1)S(1)} custom-call(s32[2]{0:T(128)S(1)} %copy-done.4, s32[16]{0:T(128)S(1)} %copy-done.5, bf16[2,256,1024]{2,1,0:T(8,128)(2,1)S(1)} %get-tuple-element.7.queries_ref, bf16[2,1280,2048]{2,1,0:T(8,128)(2,1)S(1)} %get-tuple-element.8.context_ref), custom_call_target="tpu_custom_call" | custom-call | tf_op jit(solution)/shard_map/pallas_call | solution.py:304
  68.5 0.0 copy-done
  68.5 0.0 copy-done.3
  68.5 0.0 copy-start.9
  68.5 1.3 %add_convert_fusion.1 = bf16[2,256,1024]{2,1,0:T(8,128)(2,1)S(1)} fusion(bf16[2,256,1024]{2,1,0:T(8,128)(2,1)S(1)} %copy-done.3, bf16[2,256,1024]{2,1,0:T(8,128)(2,1)S(1)} %shard_map.83, bf16[1024,1024]{1,0:T(8,128)(2,1)S(1)} %copy-done), kind=kOutput, calls=%fused_computation.3 | convolution fusion | flops 1075314688 | bytes 5242880 | tf_op jit(solution)/shard_map/spd,de->spe/dot_general | solution.py:314
  69.8 0.0 copy-start.7
  69.8 1.0 %copy-done.7 = bf16[2,256,1024]{2,1,0:T(8,128)(2,1)} copy-done((bf16[2,256,1024]{2,1,0:T(8,128)(2,1)}, bf16[2,256,1024]{2,1,0:T(8,128)(2,1)S(1)}, u32[]{:S(2)}) %copy-start.7) | copy-done | bytes 1048600
  70.8 0.0 copy-done.9
  70.8 1.5 %convolution_convert_fusion = bf16[2,256,512]{2,1,0:T(8,128)(2,1)} fusion(bf16[2,256,1024]{2,1,0:T(8,128)(2,1)S(1)} %add_convert_fusion.1, bf16[1024,512]{1,0:T(8,128)(2,1)S(1)} %copy-done.9), kind=kOutput, calls=%fused_computation.4 | convolution fusion | flops 537133056 | bytes 2621440 | tf_op jit(solution)/shard_map/spd,dc->spc/dot_general | solution.py:316
  72.3 1.5 %collective-permute-start = (bf16[2,256,512]{2,1,0:T(8,128)(2,1)}, bf16[2,256,512]{2,1,0:T(8,128)(2,1)}, u32[]{:S(2)}, u32[]{:S(2)}) collective-permute-start(bf16[2,256,512]{2,1,0:T(8,128)(2,1)} %convolution_convert_fusion), channel_id=1, source_target_pairs={{0,1},{1,0},{2,3},{3,2},{4,5},{5,4},{6,7},{7,6},{8,9},{9,8},{10,11... | collective-permute-start | bytes 1572872 | tf_op jit(solution)/shard_map/ppermute | solution.py:330
  73.8 0.0 copy-done.10
  73.8 1.9 %fusion.10 = f32[2,256,512]{2,0,1:T(2,128)S(1)} fusion(bf16[2,256,512]{2,1,0:T(8,128)(2,1)} %convolution_convert_fusion, bf16[4,4]{1,0:T(4,128)(2,1)S(1)} %copy-done.10, s32[]{:T(128)S(6)} %select_n.19), kind=kOutput, calls=%fused_computation.11 | convolution fusion | flops 1048576 | bytes 1573380 | tf_op jit(solution)/shard_map/ab,bpc->apc/dot_general | solution.py:325
  75.7 10.9 %collective-permute-done = bf16[2,256,512]{2,1,0:T(8,128)(2,1)} collective-permute-done((bf16[2,256,512]{2,1,0:T(8,128)(2,1)}, bf16[2,256,512]{2,1,0:T(8,128)(2,1)}, u32[]{:S(2)}, u32[]{:S(2)}) %collective-permute-start) | collective-permute-done | bytes 524320 | tf_op jit(solution)/shard_map/ppermute | solution.py:330
  86.6 1.8 %fusion.8 = f32[2,256,512]{2,0,1:T(2,128)S(1)} fusion(bf16[2,256,512]{2,1,0:T(8,128)(2,1)} %collective-permute-done, bf16[4,4]{1,0:T(4,128)(2,1)S(1)} %copy-done.10, s32[]{:T(128)S(6)} %select_n.19, s32[]{:T(128)S(6)} %select_n.22), kind=kOutput, calls=%fused_computation.9 | convolution fusion | flops 1048576 | bytes 1573384 | tf_op jit(solution)/shard_map/ab,bpc->apc/dot_general | solution.py:325
  88.4 0.0 copy-done.6
  88.4 0.0 copy-done.8
  88.4 1.8 %add_convert_fusion = bf16[2,256,1024]{2,1,0:T(8,128)(2,1)} fusion(bf16[2,256,1024]{2,1,0:T(8,128)(2,1)S(1)} %copy-done.8, bf16[512,1024]{1,0:T(8,128)(2,1)S(1)} %copy-done.6, f32[2,256,512]{2,0,1:T(2,128)S(1)} %fusion.8, f32[2,256,512]{2,0,1:T(2,128)S(1)} %fusion.10), kind=kOutput, calls=%fused_computation.2 | convolution fusion | flops 538968064 | bytes 5242880 | tf_op jit(solution)/shard_map/spc,cd->spd/dot_general | solution.py:333
  (7 shorter events, 0.0 us)
Async XLA Ops:
  0.0 68.5 %copy-start = (bf16[1024,1024]{1,0:T(8,128)(2,1)S(1)}, bf16[1024,1024]{1,0:T(8,128)(2,1)}, u32[]{:S(2)}) copy-start(bf16[1024,1024]{1,0:T(8,128)(2,1)} %param.12) | copy-start | bytes 6291460
  0.0 2.9 %copy-start.1 = (bf16[1024,3072]{1,0:T(8,128)(2,1)S(1)}, bf16[1024,3072]{1,0:T(8,128)(2,1)}, u32[]{:S(2)}) copy-start(bf16[1024,3072]{1,0:T(8,128)(2,1)} %weight_hbm.1) | copy-start | bytes 18874372
  2.9 1.2 %copy-start.2 = (bf16[2,256,1024]{2,1,0:T(8,128)(2,1)S(1)}, bf16[2,256,1024]{2,1,0:T(8,128)(2,1)}, u32[]{:S(2)}) copy-start(bf16[2,256,1024]{2,1,0:T(8,128)(2,1)} %history_ref.1) | copy-start | bytes 3145732
  4.2 37.5 %copy-start.4 = (s32[2]{0:T(128)S(1)}, s32[2]{0:T(128)}, u32[]{:S(2)}) copy-start(s32[2]{0:T(128)} %lengths_ref.1) | copy-start | bytes 28
  4.2 37.5 %copy-start.5 = (s32[16]{0:T(128)S(1)}, s32[16]{0:T(128)}, u32[]{:S(2)}) copy-start(s32[16]{0:T(128)} %window_ref.1) | copy-start | bytes 196
  41.7 26.8 %copy-start.3 = (bf16[2,256,1024]{2,1,0:T(8,128)(2,1)S(1)}, bf16[2,256,1024]{2,1,0:T(8,128)(2,1)}, u32[]{:S(2)}) copy-start(bf16[2,256,1024]{2,1,0:T(8,128)(2,1)} %history_ref.1) | copy-start | bytes 3145732
  68.5 2.3 %copy-start.9 = (bf16[1024,512]{1,0:T(8,128)(2,1)S(1)}, bf16[1024,512]{1,0:T(8,128)(2,1)}, u32[]{:S(2)}) copy-start(bf16[1024,512]{1,0:T(8,128)(2,1)} %param.13) | copy-start | bytes 3145732
  69.8 1.0 %copy-start.7 = (bf16[2,256,1024]{2,1,0:T(8,128)(2,1)}, bf16[2,256,1024]{2,1,0:T(8,128)(2,1)S(1)}, u32[]{:S(2)}) copy-start(bf16[2,256,1024]{2,1,0:T(8,128)(2,1)S(1)} %add_convert_fusion.1) | copy-start | bytes 3145732
  70.8 3.0 %copy-start.10 = (bf16[4,4]{1,0:T(4,128)(2,1)S(1)}, bf16[4,4]{1,0:T(4,128)(2,1)}, u32[]{:S(2)}) copy-start(bf16[4,4]{1,0:T(4,128)(2,1)} %param.15) | copy-start | bytes 100
  72.3 16.1 %copy-start.6 = (bf16[512,1024]{1,0:T(8,128)(2,1)S(1)}, bf16[512,1024]{1,0:T(8,128)(2,1)}, u32[]{:S(2)}) copy-start(bf16[512,1024]{1,0:T(8,128)(2,1)} %param.14) | copy-start | bytes 3145732
  72.3 14.3 %collective-permute-start = (bf16[2,256,512]{2,1,0:T(8,128)(2,1)}, bf16[2,256,512]{2,1,0:T(8,128)(2,1)}, u32[]{:S(2)}, u32[]{:S(2)}) collective-permute-start(bf16[2,256,512]{2,1,0:T(8,128)(2,1)} %convolution_convert_fusion), channel_id=1, source_target_pairs={{0,1},{1,0},{2,3},{3,2},{4,5},{5,4},{6,7},{7,6},{8,9},{9,8},{10,11... | collective-permute-start | bytes 1572872 | tf_op jit(solution)/shard_map/ppermute | solution.py:330
  73.8 14.6 %copy-start.8 = (bf16[2,256,1024]{2,1,0:T(8,128)(2,1)S(1)}, bf16[2,256,1024]{2,1,0:T(8,128)(2,1)}, u32[]{:S(2)}) copy-start(bf16[2,256,1024]{2,1,0:T(8,128)(2,1)} %copy-done.7) | copy-start | bytes 3145732

commit v2 on v1

v2 whole, which is shorter than its diff:
```python
import functools

import jax
import jax.numpy as jnp
from jax import lax
from jax.experimental import pallas as pl
from jax.experimental.pallas import tpu as pltpu
from jax.sharding import PartitionSpec as P

HEADS = 16
WINDOW = 512
BLOCK = 128
MASKED = -1e30
LIMIT = 46
PIECES = 4
MESH = pl.DeviceIdType.MESH


def exchange_kernel(
    history_ref, weight_hbm, queries_ref, context_ref,
    halo, weight, weight_sem, partner_send, partner_recv, y_send, y_recv,
    z_send, z_recv, x_send, x_recv, *, scale,
):
    series, rows, width = history_ref.shape
    tiles = 6
    tile = weight.shape[1] // tiles
    piece = rows // PIECES
    me = lax.axis_index("tm")
    count = lax.axis_size("tm")
    core = me % 2
    side = (me // 2) % 2
    partner = me + 1 - 2 * core
    across = me + 2 - 4 * side
    onward = me + 4 - 8 * side
    origin = me - 4 + 8 * side
    has_onward = (onward >= 0) & (onward < count)
    has_origin = (origin >= 0) & (origin < count)

    loads = [
        pltpu.make_async_copy(
            weight_hbm.at[:, pl.ds(t * tile, tile)],
            weight.at[:, pl.ds(t * tile, tile)],
            weight_sem.at[t],
        )
        for t in range(tiles)
    ]
    for load in loads[2:] + loads[:2]:
        load.start()

    barrier = pltpu.get_barrier_semaphore()
    for other in (partner, across):
        pl.semaphore_signal(barrier, inc=1, device_id={"tm": other}, device_id_type=MESH)
    for other, exists in ((onward, has_onward), (origin, has_origin)):
        @pl.when(exists)
        def _():
            pl.semaphore_signal(barrier, inc=1, device_id={"tm": other}, device_id_type=MESH)
    peers = 2 + jnp.where(has_onward, 1, 0) + jnp.where(has_origin, 1, 0)
    pl.semaphore_wait(barrier, peers)

    def remote(source, target, send, recv, device):
        return pltpu.make_async_remote_copy(
            src_ref=source, dst_ref=target, send_sem=send, recv_sem=recv,
            device_id={"tm": device}, device_id_type=MESH,
        )

    def y_copy(s, r):
        part = pl.ds(r * piece, piece)
        return remote(
            history_ref.at[s, part, :], halo.at[1, s, part, :],
            y_send.at[s, r], y_recv.at[s, r], across,
        )

    def z_copy(s, r):
        part = pl.ds(r * piece, piece)
        return remote(
            halo.at[1, s, part, :], halo.at[2, s, part, :],
            z_send.at[s, r], z_recv.at[s, r], onward,
        )

    def partner_copy(s):
        return remote(
            history_ref.at[s], halo.at[0, s], partner_send.at[s], partner_recv.at[s], partner
        )

    unit = rows // 2

    def x_copy(s, h, role):
        part = pl.ds(h * unit, unit)
        return remote(
            halo.at[role, s, part, :], halo.at[3, s, part, :],
            x_send.at[s, h], x_recv.at[s, h], partner,
        )

    for s in range(series):
        for r in range(PIECES):
            y_copy(s, r).start()
        partner_copy(s).start()

    @pl.when(jnp.logical_not(has_origin))
    def _():
        halo[2] = jnp.zeros(halo.shape[1:], halo.dtype)

    def project(source, s, slot, h=0):
        size = source.shape[0]
        first = pl.multiple_of(slot * rows + h * unit, unit)

        def body(t, _):
            column = pl.multiple_of(t * tile, tile)
            out = jnp.dot(
                source[...], weight[:, pl.ds(width + column, tile)],
                preferred_element_type=jnp.float32,
            )
            context_ref[s, pl.ds(first, size), pl.ds(column, tile)] = out.astype(jnp.bfloat16)
            return 0

        lax.fori_loop(0, 2 * width // tile, body, 0)

    def project_queries(s):
        def body(t, _):
            column = pl.multiple_of(t * tile, tile)
            out = jnp.dot(
                history_ref[s], weight[:, pl.ds(column, tile)],
                preferred_element_type=jnp.float32,
            )
            queries_ref[s, :, pl.ds(column, tile)] = out.astype(jnp.bfloat16) * scale
            return 0

        lax.fori_loop(0, width // tile, body, 0)

    def relay(s, r):
        y_copy(s, r).wait_recv()

        @pl.when(has_onward)
        def _():
            z_copy(s, r).start()

    near = core == side
    slot_partner = 3 - 2 * core
    slot_a = 4 - 4 * side
    slot_b = 4 * side
    slot_x = 1 + 2 * core

    def half_of(role, s, h):
        return halo.at[role, s, pl.ds(h * unit, unit), :]

    def finish_a(s, h):
        @pl.when(near)
        def _():
            x_copy(s, h, 1).start()
        project(half_of(1, s, h), s, slot_a, h)

    def finish_b(s, h):
        @pl.when(has_origin)
        def _():
            for r in range(h * PIECES // 2, (h + 1) * PIECES // 2):
                z_copy(s, r).wait_recv()

        @pl.when(jnp.logical_not(near))
        def _():
            x_copy(s, h, 2).start()
        project(half_of(2, s, h), s, slot_b, h)

    def finish_x(s, h):
        x_copy(s, h, 1).wait_recv()
        project(half_of(3, s, h), s, slot_x, h)

    for load in loads[2:]:
        load.wait()
    project(history_ref.at[0], 0, 2)
    for load in loads[:2]:
        load.wait()
    project_queries(0)
    relay(0, 0)
    project(history_ref.at[1], 1, 2)
    project_queries(1)
    relay(0, 1)
    for s in range(series):
        partner_copy(s).wait_recv()
        project(halo.at[0, s], s, slot_partner)
    finish_a(0, 0)
    relay(0, 2)
    relay(0, 3)
    finish_b(0, 0)
    finish_x(0, 0)
    finish_a(0, 1)
    relay(1, 0)
    finish_b(0, 1)
    finish_x(0, 1)
    relay(1, 1)
    finish_a(1, 0)
    relay(1, 2)
    finish_b(1, 0)
    finish_x(1, 0)
    relay(1, 3)
    finish_a(1, 1)
    finish_b(1, 1)
    finish_x(1, 1)

    for s in range(series):
        partner_copy(s).wait_send()
        for h in range(2):
            x_copy(s, h, 1).wait_send()
        for r in range(PIECES):
            y_copy(s, r).wait_send()

    @pl.when(has_onward)
    def _():
        for s in range(series):
            for r in range(PIECES):
                z_copy(s, r).wait_send()


def attention_kernel(
    lengths_ref, window_ref, queries_ref, context_ref, out_ref, bias_ref, weights_ref, *, s, hops
):
    rows, width = out_ref.shape
    keys = context_ref.shape[1]
    head_size = width // HEADS
    sharing = BLOCK // head_size
    pairs = width // BLOCK
    reach = WINDOW // BLOCK
    parts = rows // BLOCK
    me = lax.axis_index("tm")
    patches = rows * lax.axis_size("tm")
    first = me * rows - hops * rows
    center = hops * rows // BLOCK
    start = patches - lengths_ref[s]
    key_pos = first + lax.broadcasted_iota(jnp.int32, (1, keys), 1)
    bias_ref[...] = jnp.where((key_pos >= start) & (key_pos < patches), 0.0, MASKED)
    query_valid = me * rows + lax.broadcasted_iota(jnp.int32, (rows, BLOCK), 0) >= start
    lane = lax.broadcasted_iota(jnp.int32, (rows, BLOCK), 1)
    tilt = lax.broadcasted_iota(jnp.int32, (BLOCK, BLOCK), 1) - lax.broadcasted_iota(
        jnp.int32, (BLOCK, BLOCK), 0
    )

    def group(pair, steps):
        column = pl.multiple_of(pair * BLOCK, BLOCK)
        low = (center - steps) * BLOCK
        spots = 2 * steps + parts
        span = spots * BLOCK
        q = queries_ref[s, :, pl.ds(column, BLOCK)]
        q = jnp.concatenate(
            [jnp.where(lane // head_size == h, q, jnp.zeros_like(q)) for h in range(sharing)],
            axis=0,
        )
        k = context_ref[s, low : low + span, pl.ds(column, BLOCK)]
        scores = lax.dot_general(
            q, k, (((1,), (1,)), ((), ())), preferred_element_type=jnp.float32
        )
        for h in range(sharing):
            window = window_ref[pair * sharing + h]
            for part in range(parts):
                top_row = (h * parts + part) * BLOCK
                chunks = {}
                for spot in range(part, part + 2 * steps + 1):
                    o = spot - part - steps
                    at = spot * BLOCK
                    chunk = (
                        scores[top_row : top_row + BLOCK, at : at + BLOCK]
                        + bias_ref[:, low + at : low + at + BLOCK]
                    )
                    if o <= 0:
                        chunk = jnp.where(tilt >= -(window + o * BLOCK), chunk, MASKED)
                    if o >= 0:
                        chunk = jnp.where(tilt <= window - o * BLOCK, chunk, MASKED)
                    chunks[spot] = chunk
                top = functools.reduce(jnp.maximum, chunks.values())
                top = jnp.max(top, axis=1, keepdims=True)
                for spot in range(spots):
                    if spot in chunks:
                        value = jnp.exp(chunks[spot] - top).astype(jnp.bfloat16)
                    else:
                        value = jnp.zeros((BLOCK, BLOCK), jnp.bfloat16)
                    weights_ref[
                        top_row : top_row + BLOCK, spot * BLOCK : (spot + 1) * BLOCK
                    ] = value
        v = context_ref[s, low : low + span, pl.ds(width + column, BLOCK)]
        v = jnp.concatenate([v, jnp.ones((span, BLOCK), jnp.bfloat16)], axis=1)
        both = jnp.dot(weights_ref[:, :span], v, preferred_element_type=jnp.float32)
        both = both[:, :BLOCK] / both[:, BLOCK:]
        result = both[:rows]
        for h in range(1, sharing):
            result = jnp.where(lane // head_size == h, both[h * rows : (h + 1) * rows], result)
        out_ref[:, pl.ds(column, BLOCK)] = jnp.where(query_valid, result, 0.0).astype(jnp.bfloat16)

    def body(pair, _):
        window = window_ref[pair * sharing]
        for h in range(1, sharing):
            window = jnp.maximum(window, window_ref[pair * sharing + h])
        needed = (window + BLOCK - 1) // BLOCK
        for steps in range(1, reach + 1):
            @pl.when(needed == steps)
            def _():
                group(pair, steps)
        return 0

    lax.fori_loop(0, pairs, body, 0)


def on_device(
    history, lengths, head_window, input_proj, output_proj, mixer_down, mixer_up, series_mix
):
    series, rows, width = history.shape
    hops = -(-WINDOW // rows)
    keys = (2 * hops + 1) * rows
    head_size = width // HEADS
    vmem = pl.BlockSpec(memory_space=pltpu.VMEM)
    smem = pl.BlockSpec(memory_space=pltpu.SMEM)
    dma = pltpu.SemaphoreType.DMA
    queries, context = pl.pallas_call(
        functools.partial(exchange_kernel, scale=head_size ** (-0.5)),
        out_shape=(
            pltpu.VMEM((series, rows, width), jnp.bfloat16),
            pltpu.VMEM((series, keys, 2 * width), jnp.bfloat16),
        ),
        in_specs=[vmem, pl.BlockSpec(memory_space=pltpu.HBM)],
        out_specs=(vmem, vmem),
        scratch_shapes=[
            pltpu.VMEM((4, series, rows, width), jnp.bfloat16),
            pltpu.VMEM(input_proj.shape, jnp.bfloat16),
            dma((6,)),
            dma((series,)),
            dma((series,)),
            dma((series, PIECES)),
            dma((series, PIECES)),
            dma((series, PIECES)),
            dma((series, PIECES)),
            dma((series, 2)),
            dma((series, 2)),
        ],
        compiler_params=pltpu.CompilerParams(
            collective_id=0, has_side_effects=True, vmem_limit_bytes=LIMIT * 1024 * 1024
        ),
    )(history, input_proj)
    groups = lax.axis_size("series")
    group = lax.axis_index("series")
    mix = series_mix.astype(jnp.float32)
    hiddens = []
    combined = [0.0] * series
    for s in range(series):
        attended = pl.pallas_call(
            functools.partial(attention_kernel, s=s, hops=hops),
            out_shape=jax.ShapeDtypeStruct((rows, width), jnp.bfloat16),
            in_specs=[smem, smem, vmem, vmem],
            out_specs=vmem,
            scratch_shapes=[
                pltpu.VMEM((1, keys), jnp.float32),
                pltpu.VMEM((rows * BLOCK // head_size, keys), jnp.bfloat16),
            ],
            compiler_params=pltpu.CompilerParams(vmem_limit_bytes=32 * 1024 * 1024),
            cost_estimate=pl.CostEstimate(
                flops=8 * rows * keys * width, bytes_accessed=0, transcendentals=0
            ),
        )(lengths, head_window, queries, context)
        hidden = (
            history[s].astype(jnp.float32)
            + jnp.dot(attended, output_proj, preferred_element_type=jnp.float32)
        ).astype(jnp.bfloat16)
        hiddens.append(hidden)
        branch = jnp.dot(hidden, mixer_down, preferred_element_type=jnp.float32).astype(
            jnp.bfloat16
        )
        for offset in range(groups):
            route = [(i, (i + offset) % groups) for i in range(groups)]
            part = lax.ppermute(branch, "series", route) if offset else branch
            column = (group - offset) % groups * series + s
            for a in range(series):
                weight = lax.dynamic_slice(mix, (group * series + a, column), (1, 1))
                combined[a] = combined[a] + weight * part.astype(jnp.float32)
    outs = []
    for a in range(series):
        update = jnp.dot(
            combined[a].astype(jnp.bfloat16), mixer_up, preferred_element_type=jnp.float32
        )
        outs.append((hiddens[a].astype(jnp.float32) + update).astype(jnp.bfloat16))
    return jnp.stack(outs)


def solution(mesh):
    in_specs = (P("series", "tm", None), P("series"), P(), P(), P(), P(), P(), P())
    out_specs = P("series", "tm", None)
    return jax.shard_map(
        on_device, mesh=mesh, in_specs=in_specs, out_specs=out_specs, check_vma=False
    )
```

time: 89.5 us -> 95.2 us (1.064)
  Pallas kernels: 64.3 us -> 71.7 us
  local copies, waits for them, and re-layouts: 5.16 us -> 1.18 us
  waiting for transfers between devices: 10.9 us -> 7.26 us
  matrix products: 8.27 us -> 11.5 us
  other arithmetic: 0 us -> 1.06 us
    unnamed x22 -> x14, local copies, waits for them, and re-layouts: 5.16 us -> 0.51 us
    pallas_call x1, Pallas kernels: 37.5 us -> 41.5 us  [on_device(): pl.pallas_call(functools.partial(exchange_kernel, scale=head_size ** (-0....]
    ppermute x1 -> x2, waiting for transfers between devices: 10.9 us -> 7.26 us  [on_device(): part = lax.ppermute(branch, 'series', route) if offset else branch]
    pallas_call x1 -> x2, Pallas kernels: 26.8 us -> 30.2 us  [on_device(): pl.pallas_call(functools.partial(attention_kernel, s=s, hops=hops), out_s...]
    dot_general x5 -> x6, matrix products: 8.27 us -> 11.5 us  [the longest x2 8.47 us: on_device(): jnp.dot(combined[a].astype(jnp.bfloat16), mixer_up, preferred_element_typ...]
    another operation x0 -> x1, other arithmetic: none -> 1.06 us  [on_device(): return jnp.stack(outs)]
    ppermute x1 -> x2, starting transfers between devices: 1.49 us -> 2.09 us  [on_device(): part = lax.ppermute(branch, 'series', route) if offset else branch]
  transfers between devices with their start and end apart: 1 -> 2, of which waited for: 1 -> 1; matrix products, arithmetic and copies ran while one was open for 2% -> 3% of each run, Pallas kernels for 0% -> 16%
where the time goes in v2:
time: 95.2 us; the launch traced here: 95 us
  Pallas kernels  71.7 us (75%)
  matrix products  11.5 us (12%)
  waiting for transfers between devices  7.26 us (8%)
  starting transfers between devices  2.09 us (2%)
  local copies, waits for them, and re-layouts  1.18 us (1%)
  other arithmetic  1.06 us (1%)
    pallas_call x1, Pallas kernels, on_device(): pl.pallas_call(functools.partial(exchange_kernel, scale=head_size ** (-0....  41.5 us
    pallas_call x2, Pallas kernels, on_device(): pl.pallas_call(functools.partial(attention_kernel, s=s, hops=hops), out_s...  30.2 us
    dot_general x2, matrix products, on_device(): jnp.dot(combined[a].astype(jnp.bfloat16), mixer_up, preferred_element_typ...  8.47 us
    ppermute x2, waiting for transfers between devices, on_device(): part = lax.ppermute(branch, 'series', route) if offset else branch  7.26 us
    ppermute x2, starting transfers between devices, on_device(): part = lax.ppermute(branch, 'series', route) if offset else branch  2.09 us
  transfers between devices with their start and end apart: 2, of which 1 were waited for; matrix products, arithmetic and copies ran while one was open for 3% of the time, Pallas kernels for 16%

profile of v2, /device:TPU:4, one launch (start us, length us, event | category | flops | bytes accessed | tf_op | source)
XLA Modules:
  0.0 95.0 jit_solution(15566172844784644344)
XLA Ops:
  0.0 41.5 %shard_map.82 = (bf16[2,256,1024]{2,1,0:T(8,128)(2,1)S(1)}, bf16[2,1280,2048]{2,1,0:T(8,128)(2,1)S(1)}) custom-call(bf16[2,256,1024]{2,1,0:T(8,128)(2,1)} %history_ref.1, bf16[1024,3072]{1,0:T(8,128)(2,1)} %weight_hbm.1), custom_call_target="tpu_custom_call" | custom-call | tf_op jit(solution)/shard_map/pallas_call | solution.py:310
  41.5 0.0 copy-done.1
  41.6 0.0 copy-done.2
  41.6 0.0 copy-start.4
  41.6 15.0 %shard_map.83 = bf16[256,1024]{1,0:T(8,128)(2,1)S(1)} custom-call(s32[2]{0:T(128)S(1)} %copy-done.1, s32[16]{0:T(128)S(1)} %copy-done.2, bf16[2,256,1024]{2,1,0:T(8,128)(2,1)S(1)} %get-tuple-element.7.queries_ref, bf16[2,1280,2048]{2,1,0:T(8,128)(2,1)S(1)} %get-tuple-element.8.context_ref), custom_call_target="tpu_custom_call" | custom-call | flops 2684354560 | tf_op jit(solution)/shard_map/pallas_call | solution.py:341
  56.6 0.0 copy-done
  56.6 0.0 copy-done.4
  56.6 0.0 copy-start.3
  56.6 0.7 fusion.2
  57.4 0.5 copy-done.3
  57.8 0.4 convolution_convert_fusion.1
  58.3 1.5 %collective-permute-start = (bf16[256,512]{1,0:T(8,128)(2,1)S(1)}, bf16[256,512]{1,0:T(8,128)(2,1)}, u32[]{:S(2)}, u32[]{:S(2)}) collective-permute-start(bf16[256,512]{1,0:T(8,128)(2,1)S(1)} %convolution_convert_fusion.1), channel_id=1, source_target_pairs={{0,1},{1,0},{2,3},{3,2},{4,5},{5,4},{6,7},{7,6},{8,9},{9,8},{10,11... | collective-permute-start | bytes 786440 | tf_op jit(solution)/shard_map/ppermute | solution.py:365
  59.8 15.2 %shard_map.84 = bf16[256,1024]{1,0:T(8,128)(2,1)S(1)} custom-call(s32[2]{0:T(128)S(1)} %copy-done.1, s32[16]{0:T(128)S(1)} %copy-done.2, bf16[2,256,1024]{2,1,0:T(8,128)(2,1)S(1)} %get-tuple-element.7.queries_ref, bf16[2,1280,2048]{2,1,0:T(8,128)(2,1)S(1)} %get-tuple-element.8.context_ref), custom_call_target="tpu_custom_call" | custom-call | flops 2684354560 | tf_op jit(solution)/shard_map/pallas_call | solution.py:341
  75.0 0.0 copy-start.5
  75.0 0.7 fusion.3
  75.8 1.2 %convolution_convert_fusion = bf16[256,512]{1,0:T(8,128)(2,1)} fusion(bf16[256,1024]{1,0:T(8,128)(2,1)S(1)} %fusion.3, bf16[1024,512]{1,0:T(8,128)(2,1)S(1)} %copy-done.3), kind=kOutput, calls=%fused_computation.10 | convolution fusion | flops 268566528 | bytes 1835008 | tf_op jit(solution)/shard_map/dot_general | solution.py:360
  77.0 0.5 collective-permute-start.1
  77.5 0.0 copy-done.5
  77.5 0.7 fusion.24
  78.2 0.0 collective-permute-done
  78.2 7.3 %collective-permute-done.1 = bf16[256,512]{1,0:T(8,128)(2,1)} collective-permute-done((bf16[256,512]{1,0:T(8,128)(2,1)}, bf16[256,512]{1,0:T(8,128)(2,1)}, u32[]{:S(2)}, u32[]{:S(2)}) %collective-permute-start.1) | collective-permute-done | bytes 262176 | tf_op jit(solution)/shard_map/ppermute | solution.py:365
  85.4 4.3 %fusion.4 = bf16[1,256,1024]{2,1,0:T(8,128)(2,1)S(1)} fusion(bf16[512,1024]{1,0:T(8,128)(2,1)} %param.14, bf16[256,1024]{1,0:T(8,128)(2,1)S(1)} %fusion.3, bf16[256,512]{1,0:T(8,128)(2,1)S(1)} %convolution_convert_fusion.1, bf16[256,512]{1,0:T(8,128)(2,1)} %collective-permute-done, bf16[256,512]{1,0:T(8,128)(2,1)} %convolution_convert_fusion, ...), kind=kOutput, calls=%fused_computation.8 | convolution fusion | flops 270794752 | bytes 3145744 | tf_op jit(solution)/shard_map/dot_general | solution.py:372
  89.8 4.1 %fusion.5 = bf16[1,256,1024]{2,1,0:T(8,128)(2,1)S(1)} fusion(bf16[512,1024]{1,0:T(8,128)(2,1)S(1)} %copy-done.6, bf16[256,1024]{1,0:T(8,128)(2,1)S(1)} %fusion.2, bf16[256,512]{1,0:T(8,128)(2,1)S(1)} %convolution_convert_fusion.1, bf16[256,512]{1,0:T(8,128)(2,1)} %collective-permute-done, bf16[256,512]{1,0:T(8,128)(2,1)} %convolution_convert_fusion, ...), kind=kOutput, calls=%fused_computation.9 | convolution fusion | flops 270794752 | bytes 3145744 | tf_op jit(solution)/shard_map/dot_general | solution.py:372
  93.9 1.1 %pad_maximum_fusion = bf16[2,256,1024]{2,1,0:T(8,128)(2,1)} fusion(bf16[1,256,1024]{2,1,0:T(8,128)(2,1)S(1)} %fusion.4, bf16[1,256,1024]{2,1,0:T(8,128)(2,1)S(1)} %fusion.5), kind=kLoop, calls=%fused_computation.12 | loop fusion | flops 524288 | bytes 2097152 | tf_op jit(solution)/shard_map/stack | solution.py:376
  (5 shorter events, 0.0 us)
Async XLA Ops:
  0.0 56.6 %copy-start = (bf16[1024,1024]{1,0:T(8,128)(2,1)S(1)}, bf16[1024,1024]{1,0:T(8,128)(2,1)}, u32[]{:S(2)}) copy-start(bf16[1024,1024]{1,0:T(8,128)(2,1)} %param.12) | copy-start | bytes 6291460
  0.0 41.5 %copy-start.1 = (s32[2]{0:T(128)S(1)}, s32[2]{0:T(128)}, u32[]{:S(2)}) copy-start(s32[2]{0:T(128)} %lengths_ref.3) | copy-start | bytes 28
  0.0 41.5 %copy-start.2 = (s32[16]{0:T(128)S(1)}, s32[16]{0:T(128)}, u32[]{:S(2)}) copy-start(s32[16]{0:T(128)} %window_ref.3) | copy-start | bytes 196
  41.6 15.0 %copy-start.4 = (bf16[2,256,1024]{2,1,0:T(8,128)(2,1)S(1)}, bf16[2,256,1024]{2,1,0:T(8,128)(2,1)}, u32[]{:S(2)}) copy-start(bf16[2,256,1024]{2,1,0:T(8,128)(2,1)} %history_ref.1) | copy-start | bytes 3145732
  56.6 1.2 %copy-start.3 = (bf16[1024,512]{1,0:T(8,128)(2,1)S(1)}, bf16[1024,512]{1,0:T(8,128)(2,1)}, u32[]{:S(2)}) copy-start(bf16[1024,512]{1,0:T(8,128)(2,1)} %param.13) | copy-start | bytes 3145732
  58.3 19.9 %collective-permute-start = (bf16[256,512]{1,0:T(8,128)(2,1)S(1)}, bf16[256,512]{1,0:T(8,128)(2,1)}, u32[]{:S(2)}, u32[]{:S(2)}) collective-permute-start(bf16[256,512]{1,0:T(8,128)(2,1)S(1)} %convolution_convert_fusion.1), channel_id=1, source_target_pairs={{0,1},{1,0},{2,3},{3,2},{4,5},{5,4},{6,7},{7,6},{8,9},{9,8},{10,11... | collective-permute-start | bytes 786440 | tf_op jit(solution)/shard_map/ppermute | solution.py:365
  75.0 2.5 %copy-start.5 = (bf16[4,4]{1,0:T(4,128)(2,1)S(1)}, bf16[4,4]{1,0:T(4,128)(2,1)}, u32[]{:S(2)}) copy-start(bf16[4,4]{1,0:T(4,128)(2,1)} %param.15) | copy-start | bytes 100
  77.0 8.5 %collective-permute-start.1 = (bf16[256,512]{1,0:T(8,128)(2,1)}, bf16[256,512]{1,0:T(8,128)(2,1)}, u32[]{:S(2)}, u32[]{:S(2)}) collective-permute-start(bf16[256,512]{1,0:T(8,128)(2,1)} %convolution_convert_fusion), channel_id=1, source_target_pairs={{0,1},{1,0},{2,3},{3,2},{4,5},{5,4},{6,7},{7,6},{8,9},{9,8},{10,11... | collective-permute-start | bytes 786440 | tf_op jit(solution)/shard_map/ppermute | solution.py:365
  77.5 12.3 %copy-start.6 = (bf16[512,1024]{1,0:T(8,128)(2,1)S(1)}, bf16[512,1024]{1,0:T(8,128)(2,1)}, u32[]{:S(2)}) copy-start(bf16[512,1024]{1,0:T(8,128)(2,1)} %param.14) | copy-start | bytes 3145732

commit v3 on v2

--- a/solution.py
+++ b/solution.py
@@ -211,7 +211,7 @@
 
 
 def attention_kernel(
-    lengths_ref, window_ref, queries_ref, context_ref, out_ref, bias_ref, weights_ref, *, s, hops
+    lengths_ref, window_ref, queries_ref, context_ref, out_ref, bias_ref, *, s, hops
 ):
     rows, width = out_ref.shape
     keys = context_ref.shape[1]
@@ -233,68 +233,72 @@
         jnp.int32, (BLOCK, BLOCK), 0
     )
 
-    def group(pair, steps):
+    mine = [lane[:BLOCK] // head_size == h for h in range(sharing)]
+
+    def one_head(pair, h, steps, window):
         column = pl.multiple_of(pair * BLOCK, BLOCK)
-        low = (center - steps) * BLOCK
-        spots = 2 * steps + parts
-        span = spots * BLOCK
-        q = queries_ref[s, :, pl.ds(column, BLOCK)]
-        q = jnp.concatenate(
-            [jnp.where(lane // head_size == h, q, jnp.zeros_like(q)) for h in range(sharing)],
-            axis=0,
-        )
-        k = context_ref[s, low : low + span, pl.ds(column, BLOCK)]
-        scores = lax.dot_general(
-            q, k, (((1,), (1,)), ((), ())), preferred_element_type=jnp.float32
-        )
-        for h in range(sharing):
-            window = window_ref[pair * sharing + h]
-            for part in range(parts):
-                top_row = (h * parts + part) * BLOCK
-                chunks = {}
-                for spot in range(part, part + 2 * steps + 1):
-                    o = spot - part - steps
-                    at = spot * BLOCK
-                    chunk = (
-                        scores[top_row : top_row + BLOCK, at : at + BLOCK]
-                        + bias_ref[:, low + at : low + at + BLOCK]
-                    )
+        span = (2 * steps + 1) * BLOCK
+        for part in range(parts):
+            low = (center + part - steps) * BLOCK
+            q = queries_ref[s, part * BLOCK : (part + 1) * BLOCK, pl.ds(column, BLOCK)]
+            q = jnp.where(mine[h], q, jnp.zeros_like(q))
+            k = context_ref[s, low : low + span, pl.ds(column, BLOCK)]
+            scores = lax.dot_general(
+                q, k, (((1,), (1,)), ((), ())), preferred_element_type=jnp.float32
+            )
+            chunks = []
+            for o in range(-steps, steps + 1):
+                at = (o + steps) * BLOCK
+                chunk = scores[:, at : at + BLOCK] + bias_ref[:, low + at : low + at + BLOCK]
+                if abs(o) >= steps - 1:
                     if o <= 0:
                         chunk = jnp.where(tilt >= -(window + o * BLOCK), chunk, MASKED)
                     if o >= 0:
                         chunk = jnp.where(tilt <= window - o * BLOCK, chunk, MASKED)
-                    chunks[spot] = chunk
-                top = functools.reduce(jnp.maximum, chunks.values())
-                top = jnp.max(top, axis=1, keepdims=True)
-                for spot in range(spots):
-                    if spot in chunks:
-                        value = jnp.exp(chunks[spot] - top).astype(jnp.bfloat16)
-                    else:
-                        value = jnp.zeros((BLOCK, BLOCK), jnp.bfloat16)
-                    weights_ref[
-                        top_row : top_row + BLOCK, spot * BLOCK : (spot + 1) * BLOCK
-                    ] = value
-        v = context_ref[s, low : low + span, pl.ds(width + column, BLOCK)]
-        v = jnp.concatenate([v, jnp.ones((span, BLOCK), jnp.bfloat16)], axis=1)
-        both = jnp.dot(weights_ref[:, :span], v, preferred_element_type=jnp.float32)
-        both = both[:, :BLOCK] / both[:, BLOCK:]
-        result = both[:rows]
-        for h in range(1, sharing):
-            result = jnp.where(lane // head_size == h, both[h * rows : (h + 1) * rows], result)
-        out_ref[:, pl.ds(column, BLOCK)] = jnp.where(query_valid, result, 0.0).astype(jnp.bfloat16)
+                chunks.append(chunk)
+            top = functools.reduce(jnp.maximum, chunks)
+            top = jnp.max(top, axis=1, keepdims=True)
+            weights = jnp.concatenate(
+                [jnp.exp(chunk - top).astype(jnp.bfloat16) for chunk in chunks], axis=1
+            )
+            v = context_ref[s, low : low + span, pl.ds(width + column, BLOCK)]
+            v = jnp.concatenate([v, jnp.ones((span, BLOCK), jnp.bfloat16)], axis=1)
+            both = jnp.dot(weights, v, preferred_element_type=jnp.float32)
+            result = both[:, :BLOCK] / both[:, BLOCK:]
+            valid = query_valid[part * BLOCK : (part + 1) * BLOCK]
+            result = jnp.where(valid, result, 0.0).astype(jnp.bfloat16)
+            place = (slice(part * BLOCK, (part + 1) * BLOCK), pl.ds(column, BLOCK))
+            if h:
+                result = jnp.where(mine[h], result, out_ref[place])
+            out_ref[place] = result
 
     def body(pair, _):
-        window = window_ref[pair * sharing]
-        for h in range(1, sharing):
-            window = jnp.maximum(window, window_ref[pair * sharing + h])
-        needed = (window + BLOCK - 1) // BLOCK
-        for steps in range(1, reach + 1):
-            @pl.when(needed == steps)
-            def _():
-                group(pair, steps)
+        for h in range(sharing):
+            window = window_ref[pair * sharing + h]
+            needed = (window + BLOCK - 1) // BLOCK
+            for steps in range(1, reach + 1):
+                @pl.when(needed == steps)
+                def _():
+                    one_head(pair, h, steps, window)
         return 0
 
     lax.fori_loop(0, pairs, body, 0)
+
+
+def mixing_kernel(mix_ref, up_ref, *refs, series, groups):
+    hiddens, parts, out_ref = refs[:series], refs[series:-1], refs[-1]
+    group = lax.axis_index("series")
+    for a in range(series):
+        total = None
+        for index, part in enumerate(parts):
+            offset = index % groups
+            column = lax.rem(group - offset + groups, groups) * series + index // groups
+            term = mix_ref[group * series + a, column] * part[...].astype(jnp.float32)
+            total = term if total is None else total + term
+        update = jnp.dot(
+            total.astype(jnp.bfloat16), up_ref[...], preferred_element_type=jnp.float32
+        )
+        out_ref[a] = (hiddens[a][...].astype(jnp.float32) + update).astype(jnp.bfloat16)
 
 
 def on_device(
@@ -333,10 +337,9 @@
         ),
     )(history, input_proj)
     groups = lax.axis_size("series")
-    group = lax.axis_index("series")
     mix = series_mix.astype(jnp.float32)
     hiddens = []
-    combined = [0.0] * series
+    parts = []
     for s in range(series):
         attended = pl.pallas_call(
             functools.partial(attention_kernel, s=s, hops=hops),
@@ -345,7 +348,6 @@
             out_specs=vmem,
             scratch_shapes=[
                 pltpu.VMEM((1, keys), jnp.float32),
-                pltpu.VMEM((rows * BLOCK // head_size, keys), jnp.bfloat16),
             ],
             compiler_params=pltpu.CompilerParams(vmem_limit_bytes=32 * 1024 * 1024),
             cost_estimate=pl.CostEstimate(
@@ -362,18 +364,14 @@
         )
         for offset in range(groups):
             route = [(i, (i + offset) % groups) for i in range(groups)]
-            part = lax.ppermute(branch, "series", route) if offset else branch
-            column = (group - offset) % groups * series + s
-            for a in range(series):
-                weight = lax.dynamic_slice(mix, (group * series + a, column), (1, 1))
-                combined[a] = combined[a] + weight * part.astype(jnp.float32)
-    outs = []
-    for a in range(series):
-        update = jnp.dot(
-            combined[a].astype(jnp.bfloat16), mixer_up, preferred_element_type=jnp.float32
-        )
-        outs.append((hiddens[a].astype(jnp.float32) + update).astype(jnp.bfloat16))
-    return jnp.stack(outs)
+            parts.append(lax.ppermute(branch, "series", route) if offset else branch)
+    return pl.pallas_call(
+        functools.partial(mixing_kernel, series=series, groups=groups),
+        out_shape=jax.ShapeDtypeStruct(history.shape, jnp.bfloat16),
+        in_specs=[smem, vmem] + [vmem] * (len(hiddens) + len(parts)),
+        out_specs=vmem,
+        compiler_params=pltpu.CompilerParams(vmem_limit_bytes=32 * 1024 * 1024),
+    )(mix, mixer_up, *hiddens, *parts)
 
 
 def solution(mesh):

time: 95.2 us -> 83.6 us (0.88); the launches traced: 95 us -> 85 us
  matrix products: 11.5 us -> 2.33 us
  other arithmetic: 1.06 us -> 0.01 us
    dot_general x2 -> x0, matrix products: 8.47 us -> none  [on_device(): jnp.dot(combined[a].astype(jnp.bfloat16), mixer_up, preferred_element_typ...]
    pallas_call x0 -> x1, Pallas kernels: none -> 2.46 us  [on_device(): pl.pallas_call(functools.partial(mixing_kernel, series=series, groups=gro...]
    pallas_call x2, Pallas kernels: 30.2 us -> 28.5 us  [on_device(): pl.pallas_call(functools.partial(attention_kernel, s=s, hops=hops), out_s...]
    another operation x1 -> x0, other arithmetic: 1.06 us -> none  [on_device(): return jnp.stack(outs)]
  transfers between devices with their start and end apart: 2 -> 2, of which waited for: 1 -> 1; matrix products, arithmetic and copies ran while one was open for 3% -> 1% of each run, Pallas kernels for 16% -> 17%
where the time goes in v3:
time: 83.6 us; the launch traced here: 85 us
  Pallas kernels  72.2 us (86%)
  waiting for transfers between devices  7.64 us (9%)
  matrix products  2.33 us (3%)
  starting transfers between devices  2.16 us (3%)
    pallas_call x1, Pallas kernels, on_device(): pl.pallas_call(functools.partial(exchange_kernel, scale=head_size ** (-0....  41.2 us
    pallas_call x2, Pallas kernels, on_device(): pl.pallas_call(functools.partial(attention_kernel, s=s, hops=hops), out_s...  28.5 us
    ppermute x2, waiting for transfers between devices, on_device(): parts.append(lax.ppermute(branch, 'series', route) if offset else branch)  7.64 us
    pallas_call x1, Pallas kernels, on_device(): pl.pallas_call(functools.partial(mixing_kernel, series=series, groups=gro...  2.46 us
    ppermute x2, starting transfers between devices, on_device(): parts.append(lax.ppermute(branch, 'series', route) if offset else branch)  2.16 us
  transfers between devices with their start and end apart: 2, of which 1 were waited for; matrix products, arithmetic and copies ran while one was open for 1% of the time, Pallas kernels for 17%

profile of v3, /device:TPU:4, one launch (start us, length us, event | category | flops | bytes accessed | tf_op | source)
XLA Modules:
  0.0 85.0 jit_solution(9923466824862580134)
XLA Ops:
  0.0 0.0 copy-start
  0.0 41.2 %shard_map.82 = (bf16[2,256,1024]{2,1,0:T(8,128)(2,1)S(1)}, bf16[2,1280,2048]{2,1,0:T(8,128)(2,1)S(1)}) custom-call(bf16[2,256,1024]{2,1,0:T(8,128)(2,1)} %history_ref.1, bf16[1024,3072]{1,0:T(8,128)(2,1)} %weight_hbm.1), custom_call_target="tpu_custom_call" | custom-call | tf_op jit(solution)/shard_map/pallas_call | solution.py:314
  41.3 0.0 copy-done.3
  41.3 0.0 copy-done.2
  41.3 0.0 copy-start.5
  41.3 14.2 %shard_map.83 = bf16[256,1024]{1,0:T(8,128)(2,1)S(1)} custom-call(s32[2]{0:T(128)S(1)} %copy-done.2, s32[16]{0:T(128)S(1)} %copy-done.3, bf16[2,256,1024]{2,1,0:T(8,128)(2,1)S(1)} %get-tuple-element.7.queries_ref, bf16[2,1280,2048]{2,1,0:T(8,128)(2,1)S(1)} %get-tuple-element.8.context_ref), custom_call_target="tpu_custom_call" | custom-call | flops 2684354560 | tf_op jit(solution)/shard_map/pallas_call | solution.py:344
  55.5 0.0 copy-done
  55.5 0.0 copy-done.5
  55.5 0.0 copy-start.4
  55.5 0.7 fusion.refs_0_
  56.3 0.5 copy-done.4
  56.7 0.4 convolution_convert_fusion.1.refs_2_
  57.2 1.6 %collective-permute-start = (bf16[256,512]{1,0:T(8,128)(2,1)S(1)}, bf16[256,512]{1,0:T(8,128)(2,1)S(1)}, u32[]{:S(2)}, u32[]{:S(2)}) collective-permute-start(bf16[256,512]{1,0:T(8,128)(2,1)S(1)} %convolution_convert_fusion.1.refs_2_), channel_id=1, source_target_pairs={{0,1},{1,0},{2,3},{3,2},{4,5},{5,4},{6,7},{7,6},{8,9},{9,8},{10,11... | collective-permute-start | bytes 786440 | tf_op jit(solution)/shard_map/ppermute | solution.py:367
  58.7 14.4 %shard_map.84 = bf16[256,1024]{1,0:T(8,128)(2,1)S(1)} custom-call(s32[2]{0:T(128)S(1)} %copy-done.2, s32[16]{0:T(128)S(1)} %copy-done.3, bf16[2,256,1024]{2,1,0:T(8,128)(2,1)S(1)} %get-tuple-element.7.queries_ref, bf16[2,1280,2048]{2,1,0:T(8,128)(2,1)S(1)} %get-tuple-element.8.context_ref), custom_call_target="tpu_custom_call" | custom-call | flops 2684354560 | tf_op jit(solution)/shard_map/pallas_call | solution.py:344
  73.1 0.0 copy-start.6
  73.1 0.0 copy-start.1
  73.1 0.7 fusion.1.refs_1_
  73.9 0.4 convolution_convert_fusion.refs_4_
  74.3 0.6 collective-permute-start.1
  74.9 0.0 copy-done.6
  74.9 0.0 collective-permute-done.refs_3_
  74.9 7.6 %collective-permute-done.1.refs_5_ = bf16[256,512]{1,0:T(8,128)(2,1)S(1)} collective-permute-done((bf16[256,512]{1,0:T(8,128)(2,1)S(1)}, bf16[256,512]{1,0:T(8,128)(2,1)S(1)}, u32[]{:S(2)}, u32[]{:S(2)}) %collective-permute-start.1) | collective-permute-done | bytes 262176 | tf_op jit(solution)/shard_map/ppermute | solution.py:367
  82.6 0.0 copy-done.1
  82.6 2.5 %shard_map.85 = bf16[2,256,1024]{2,1,0:T(8,128)(2,1)} custom-call(f32[4,4]{1,0:T(4,128)S(1)} %convert_element_type.27.mix_ref, bf16[512,1024]{1,0:T(8,128)(2,1)S(1)} %copy-done.1, bf16[256,1024]{1,0:T(8,128)(2,1)S(1)} %fusion.refs_0_, bf16[256,1024]{1,0:T(8,128)(2,1)S(1)} %fusion.1.refs_1_, bf16[256,512]{1,0:T(8,128)(2,1)S(1)} %convolution_convert_fusion.1.refs_2_, ...), custom_call_target="tpu_custom_call" | custom-call | tf_op jit(solution)/shard_map/pallas_call | solution.py:368
  (3 shorter events, 0.0 us)
Async XLA Ops:
  0.0 55.5 %copy-start = (bf16[1024,1024]{1,0:T(8,128)(2,1)S(1)}, bf16[1024,1024]{1,0:T(8,128)(2,1)}, u32[]{:S(2)}) copy-start(bf16[1024,1024]{1,0:T(8,128)(2,1)} %param.12) | copy-start | bytes 6291460
  0.0 41.3 %copy-start.3 = (s32[16]{0:T(128)S(1)}, s32[16]{0:T(128)}, u32[]{:S(2)}) copy-start(s32[16]{0:T(128)} %window_ref.3) | copy-start | bytes 196
  0.0 41.3 %copy-start.2 = (s32[2]{0:T(128)S(1)}, s32[2]{0:T(128)}, u32[]{:S(2)}) copy-start(s32[2]{0:T(128)} %lengths_ref.3) | copy-start | bytes 28
  41.3 14.2 %copy-start.5 = (bf16[2,256,1024]{2,1,0:T(8,128)(2,1)S(1)}, bf16[2,256,1024]{2,1,0:T(8,128)(2,1)}, u32[]{:S(2)}) copy-start(bf16[2,256,1024]{2,1,0:T(8,128)(2,1)} %history_ref.1) | copy-start | bytes 3145732
  55.5 1.2 %copy-start.4 = (bf16[1024,512]{1,0:T(8,128)(2,1)S(1)}, bf16[1024,512]{1,0:T(8,128)(2,1)}, u32[]{:S(2)}) copy-start(bf16[1024,512]{1,0:T(8,128)(2,1)} %param.13) | copy-start | bytes 3145732
  57.2 17.7 %collective-permute-start = (bf16[256,512]{1,0:T(8,128)(2,1)S(1)}, bf16[256,512]{1,0:T(8,128)(2,1)S(1)}, u32[]{:S(2)}, u32[]{:S(2)}) collective-permute-start(bf16[256,512]{1,0:T(8,128)(2,1)S(1)} %convolution_convert_fusion.1.refs_2_), channel_id=1, source_target_pairs={{0,1},{1,0},{2,3},{3,2},{4,5},{5,4},{6,7},{7,6},{8,9},{9,8},{10,11... | collective-permute-start | bytes 786440 | tf_op jit(solution)/shard_map/ppermute | solution.py:367
  73.1 1.8 %copy-start.6 = (bf16[4,4]{1,0:T(4,128)(2,1)S(1)}, bf16[4,4]{1,0:T(4,128)(2,1)}, u32[]{:S(2)}) copy-start(bf16[4,4]{1,0:T(4,128)(2,1)} %param.15) | copy-start | bytes 100
  73.1 9.4 %copy-start.1 = (bf16[512,1024]{1,0:T(8,128)(2,1)S(1)}, bf16[512,1024]{1,0:T(8,128)(2,1)}, u32[]{:S(2)}) copy-start(bf16[512,1024]{1,0:T(8,128)(2,1)} %up_ref.1) | copy-start | bytes 3145732
  74.3 8.2 %collective-permute-start.1 = (bf16[256,512]{1,0:T(8,128)(2,1)S(1)}, bf16[256,512]{1,0:T(8,128)(2,1)S(1)}, u32[]{:S(2)}, u32[]{:S(2)}) collective-permute-start(bf16[256,512]{1,0:T(8,128)(2,1)S(1)} %convolution_convert_fusion.refs_4_), channel_id=1, source_target_pairs={{0,1},{1,0},{2,3},{3,2},{4,5},{5,4},{6,7},{7,6},{8,9},{9,8},{10,11... | collective-permute-start | bytes 786440 | tf_op jit(solution)/shard_map/ppermute | solution.py:367
